TPU v7x, 32 devices: a 4x4x1 block of a 4x4x8 slice. The times are simulated.
32 devices in a mesh: dp: 1 (over z), tp: 32 (over x, y, core).
Axes of the slice: x: 4, y: 4, z: 1, core: 2. Of those that a mesh axis runs over, the one named last changes fastest.
The devices are a block of a 4x4x8 slice.
Arguments:
- x: bfloat16 [8192, 4608], P(('dp', 'tp'))
- w_gate: bfloat16 [4608, 36864], P(None, 'tp')
- w_up: bfloat16 [4608, 36864], P(None, 'tp')
- w_down: bfloat16 [36864, 4608], P('tp')
Outputs:
- output: bfloat16 [8192, 4608], P(('dp', 'tp'))
All inputs are finite; a program needn't handle non-finite values.
Results may differ from a plain program's by a relative error of at most 0.016.
Values are sent between devices in bfloat16 or wider.
A program may use at most 768 MiB of HBM per device.

v0:
```python
import jax
import jax.numpy as jnp
from jax import lax
from jax.sharding import PartitionSpec as P


def solution(mesh):
    def step(x, w_gate, w_up, w_down):
        rows = lax.all_gather(x, "tp", axis=0, tiled=True)
        gate = jnp.dot(rows, w_gate, preferred_element_type=jnp.float32)
        up = jnp.dot(rows, w_up, preferred_element_type=jnp.float32)
        hidden = (jax.nn.gelu(gate) * up).astype(jnp.bfloat16)
        term = jnp.dot(hidden, w_down, preferred_element_type=jnp.float32).astype(jnp.bfloat16)
        return lax.psum_scatter(term, "tp", scatter_dimension=0, tiled=True)

    return jax.shard_map(
        step,
        mesh=mesh,
        in_specs=(P(("dp", "tp"), None), P(None, "tp"), P(None, "tp"), P("tp", None)),
        out_specs=P(("dp", "tp"), None),
        check_vma=False,
    )
```

profile of v0, /device:TPU:97, one launch (start us, length us, event | category | flops | bytes accessed | tf_op | source)
XLA Modules:
  0.0 874.6 jit_solution(12940443099308669682)
XLA Ops:
  6.5 0.0 all-gather.2.cloned.1.call-start
  6.6 0.7 all-gather.2.cloned.1.call-update
  7.3 0.1 reduce-scatter.4.cloned.1.call-start
  7.4 224.0 %all-gather.2.cloned.1.call-done = bf16[8192,4608]{1,0:T(8,128)(2,1)} async-done(((bf16[256,4608]{1,0:T(8,128)(2,1)}), bf16[8192,4608]{1,0:T(8,128)(2,1)}) %all-gather.2.cloned.1.call-update) | async-done | bytes 75497488 | tf_op jit(solution)/shard_map/all_gather | solution.py:9
  231.4 107.3 %fusion.8 = f32[8192,1152]{1,0:T(8,128)} fusion(bf16[8192,4608]{1,0:T(8,128)(2,1)} %all-gather.2.cloned.1.call-done, bf16[4608,1152]{1,0:T(8,128)(2,1)} %param.5), kind=kOutput, calls=%fused_computation.11 | convolution fusion | flops 86973087744 | bytes 123863040 | tf_op jit(solution)/shard_map/dot_general | solution.py:10
  338.8 111.7 %fusion.7 = bf16[8192,1152]{1,0:T(8,128)(2,1)} fusion(bf16[8192,4608]{1,0:T(8,128)(2,1)} %all-gather.2.cloned.1.call-done, bf16[4608,1152]{1,0:T(8,128)(2,1)} %param.6, f32[8192,1152]{1,0:T(8,128)} %fusion.8), kind=kOutput, calls=%fused_computation.10 | convolution fusion | flops 87067459584 | bytes 142737408 | tf_op jit(solution)/shard_map/dot_general | solution.py:11
  450.5 107.0 %convolution_convert_fusion = bf16[8192,4608]{1,0:T(8,128)(2,1)} fusion(bf16[8192,1152]{1,0:T(8,128)(2,1)} %fusion.7, bf16[1152,4608]{1,0:T(8,128)(2,1)} %param.7), kind=kOutput, calls=%fused_computation | convolution fusion | flops 87010836480 | bytes 104988672 | tf_op jit(solution)/shard_map/dot_general | solution.py:13
  557.5 0.1 reduce-scatter.4.cloned.1.call-update
  557.6 310.1 %reduce-scatter.4.cloned.1.call-done = bf16[256,4608]{1,0:T(8,128)(2,1)} async-done(((bf16[8192,4608]{1,0:T(8,128)(2,1)}), bf16[256,4608]{1,0:T(8,128)(2,1)}) %reduce-scatter.4.cloned.1.call-update) | async-done | bytes 2359312
Async XLA Ops:
  6.5 224.9 %all-gather.2.cloned.1.call-start = ((), (), s32[]{:S(2)}) async-start(), calls=%async_computation.1 | async-start | bytes 77856768 | tf_op jit(solution)/shard_map/all_gather | solution.py:9
  7.3 860.4 %reduce-scatter.4.cloned.1.call-start = ((), (), s32[]{:S(2)}) async-start(), calls=%async_computation.2 | async-start | bytes 77856768
Sparse Core Ops, SparseCore 0:
  9.4 221.9 all-gather.1
  557.7 309.9 reduce-scatter.3
where the time goes:
time: 875 us
  waiting for transfers between devices  535 us (61%)
  matrix products  326 us (37%)
  between operations  13.4 us (2%)
    unnamed x3, waiting for transfers between devices  311 us
    all_gather x1, waiting for transfers between devices, step(): rows = lax.all_gather(x, 'tp', axis=0, tiled=True)  224 us
    dot_general x1, matrix products, step(): up = jnp.dot(rows, w_up, preferred_element_type=jnp.float32)  112 us
    dot_general x1, matrix products, step(): gate = jnp.dot(rows, w_gate, preferred_element_type=jnp.float32)  107 us
    dot_general x1, matrix products, step(): jnp.dot(hidden, w_down, preferred_element_type=jnp.float32)  107 us
  transfers between devices with their start and end apart: 2, of which 2 were waited for; matrix products, arithmetic and copies ran while one was open for 0% of the time, Pallas kernels for 0%

commit v1 on v0

v1 whole, which is shorter than its diff:
```python
import functools
import math

import jax
import jax.numpy as jnp
from jax import lax
from jax.experimental import pallas as pl
from jax.experimental.pallas import tpu as pltpu
from jax.sharding import PartitionSpec as P

MESH = pl.DeviceIdType.MESH
BF16, F32 = jnp.bfloat16, jnp.float32
ANY = pl.BlockSpec(memory_space=pl.ANY)
LIMIT = 67043328

ORDER = (
    (0, 0), (0, -1), (0, 1), (-1, 0), (1, 0), (0, 2), (-1, -1), (1, -1),
    (-1, 1), (1, 1), (-1, 2), (1, 2), (2, 0), (2, 1), (2, -1), (2, 2),
)
SLOT = {place: i for i, place in enumerate(ORDER)}
SECOND_HALF = len(ORDER)


def pick(index, values):
    out = jnp.int32(values[0])
    for i, v in enumerate(values[1:], 1):
        out = jnp.where(index == i, jnp.int32(v), out)
    return out


class Place:
    def __init__(self, n):
        t = lax.axis_index("tp")
        self.n = n
        self.core = lax.rem(t, 2)
        self.partner = t + 1 - 2 * self.core
        self.y = lax.rem(lax.div(t, 2), n)
        self.x = lax.div(t, 2 * n)

    def gf(self, half, rg=0, rf=0):
        g, f = (self.x, self.y) if half == 0 else (self.y, self.x)
        return lax.rem(g + rg + self.n, self.n), lax.rem(f + rf + self.n, self.n)

    def device(self, half, rg, rf):
        g, f = self.gf(half, rg, rf)
        x, y = (g, f) if half == 0 else (f, g)
        return (x * self.n + y) * 2 + self.core


def remote(src, dst, send, recv, device):
    return pltpu.make_async_remote_copy(
        src_ref=src, dst_ref=dst, send_sem=send, recv_sem=recv, device_id={"tp": device}, device_id_type=MESH
    )


def greet(devices):
    barrier = pltpu.get_barrier_semaphore()
    for d in devices:
        pl.semaphore_signal(barrier, inc=1, device_id={"tp": d}, device_id_type=MESH)
    pl.semaphore_wait(barrier, len(devices))


def gather_kernel(
    n, x, wg, wu, wd, xg, hf, wdp,
    wv, xb, hb, send, recv, psend, precv, wsem, xsem, hsend, hlocal, hrecv, dsem,
):
    me = Place(n)
    c = me.core
    rows, depth = x.shape
    u = rows // 2
    units = wg.shape[1]
    tiles = units // 128

    def block(owner_core, half, rg, rf):
        g, f = me.gf(half, rg, rf)
        return xg.at[owner_core, half, g, f]

    counts = []

    def push(src, dst, half, device, slot):
        k = len(counts)
        counts.append(src)
        remote(src, dst, send.at[k], recv.at[half, slot], device).start()

    halves_sent = []

    def own(half):
        return x.at[pl.ds(half * u, u)]

    def forward(half, place):
        rg, rf = place
        mine = block(c, half, rg, rf)
        if place == (0, 0):
            src = own(half)
            push(src, mine, half, me.device(half, 0, 1), SLOT[(0, -1)])
            push(src, mine, half, me.device(half, 0, -1), SLOT[(0, 1)])
            push(src, mine, half, me.device(half, 1, 0), SLOT[(-1, 0)])
            push(src, mine, half, me.device(half, -1, 0), SLOT[(1, 0)])
        else:
            src = mine
        if place == (0, -1):
            part = mine.at[pl.ds(0, u // 2)]
            halves_sent.append(len(counts))
            push(part, part, half, me.device(half, 0, 1), SLOT[(0, 2)])
        if place == (0, 1):
            part = mine.at[pl.ds(u // 2, u // 2)]
            halves_sent.append(len(counts))
            push(part, part, half, me.device(half, 0, -1), SECOND_HALF)
        if rg == 0 and rf != 0:
            push(mine, mine, half, me.device(half, 1, 0), SLOT[(-1, rf)])
            push(mine, mine, half, me.device(half, -1, 0), SLOT[(1, rf)])
        if rg == -1 and rf in (0, -1):
            push(mine, mine, half, me.device(half, 1, 0), SLOT[(2, rf)])
        if rg == 1 and rf in (1, 2):
            push(mine, mine, half, me.device(half, -1, 0), SLOT[(2, rf)])
        remote(src, mine, psend.at[half, SLOT[place]], precv.at[half, SLOT[place]], me.partner).start()

    def arrived(half, place):
        mine = block(c, half, *place)
        if place == (0, 2):
            for slot, lo in ((SLOT[place], 0), (SECOND_HALF, u // 2)):
                part = mine.at[pl.ds(lo, u // 2)]
                remote(part, part, send.at[0], recv.at[half, slot], me.partner).wait_recv()
        else:
            remote(mine, mine, send.at[0], recv.at[half, SLOT[place]], me.partner).wait_recv()

    def handed_over(half, slot, rg, rf):
        theirs = block(1 - c, half, rg, rf)
        remote(theirs, theirs, send.at[0], precv.at[half, slot], me.partner).wait_recv()

    def tile_rows(core, half):
        return pl.ds(pl.multiple_of((core * 2 + half) * u, u), u)

    def tile_copy(slot, core, half, rg, rf):
        return pltpu.make_async_copy(
            block(core, half, rg, rf), xb.at[slot, tile_rows(core, half)], xsem.at[slot, core, half]
        )

    greet(
        [me.partner]
        + [me.device(0, rg, rf) for rg, rf in ((0, 1), (0, -1), (1, 0), (-1, 0))]
    )
    for half in (0, 1):
        forward(half, (0, 0))
    for half in (0, 1):
        pltpu.make_async_copy(own(half), xb.at[0, tile_rows(c, half)], xsem.at[0, c, half]).start()

    def weights(j, part):
        w = (wg, wu)[part]
        return pltpu.make_async_copy(
            w.at[:, pl.ds(pl.multiple_of(j * 128, 128), 128)],
            wv.at[j, :, pl.ds(part * 128, 128)],
            wsem.at[j, part],
        )

    def start_weights(j, carry):
        weights(j, 0).start()
        weights(j, 1).start()
        return carry

    lax.fori_loop(0, tiles, start_weights, 0)
    for half in (0, 1):
        handed_over(half, 0, 0, 0)
        tile_copy(0, 1 - c, half, 0, 0).start()
    down = remote(wd, wdp, dsem.at[0], dsem.at[1], me.partner)
    down.start()

    look, fetch = tiles // 3, (2 * tiles) // 3
    steps = len(ORDER)

    def offsets(s):
        return pick(s, [p[0] for p in ORDER]), pick(s, [p[1] for p in ORDER])

    def hidden_copies(slot, half, rg, rf):
        g, f = me.gf(half, rg, rf)
        mine = pltpu.make_async_copy(
            hb.at[slot, tile_rows(c, half)], hf.at[c, half, g, f], hlocal.at[slot, half]
        )
        theirs = remote(
            hb.at[slot, tile_rows(1 - c, half)], hf.at[c, half, g, f], hsend.at[slot, half], hrecv.at[0], me.partner
        )
        return mine, theirs

    def step(s, carry):
        slot = lax.rem(s, 2)
        rg, rf = offsets(s)
        ng, nf = offsets(s + 1)
        for core in (0, 1):
            for half in (0, 1):
                tile_copy(slot, core, half, rg, rf).wait()

        @pl.when(s >= 2)
        def _():
            for half in (0, 1):
                mine, theirs = hidden_copies(slot, half, rg, rf)
                mine.wait()
                theirs.wait_send()

        def tile(j, carry):
            @pl.when(s == 0)
            def _():
                weights(j, 0).wait()
                weights(j, 1).wait()

            @pl.when(j == look)
            def _():
                for k in range(1, steps):

                    @pl.when(s == k - 1)
                    def _():
                        for half in (0, 1):
                            arrived(half, ORDER[k])
                            forward(half, ORDER[k])

            @pl.when((j == fetch) & (s < steps - 1))
            def _():
                for half in (0, 1):
                    tile_copy(1 - slot, c, half, ng, nf).start()
                for half in (0, 1):
                    handed_over(half, s + 1, ng, nf)
                    tile_copy(1 - slot, 1 - c, half, ng, nf).start()

            both = jnp.dot(xb[slot], wv[j], preferred_element_type=F32)
            gate, up = both[:, :128], both[:, 128:]
            hb[slot, :, pl.ds(pl.multiple_of(j * 128, 128), 128)] = (jax.nn.gelu(gate) * up).astype(BF16)
            return carry

        lax.fori_loop(0, tiles, tile, 0)
        for half in (0, 1):
            mine, theirs = hidden_copies(slot, half, rg, rf)
            mine.start()
            theirs.start()
        return carry

    lax.fori_loop(0, steps, step, 0)

    for slot in (0, 1):
        for half in (0, 1):
            mine, theirs = hidden_copies(slot, half, 0, 0)
            mine.wait()
            theirs.wait_send()
    landed = hf.at[1 - c]
    remote(landed, landed, send.at[0], hrecv.at[0], me.partner).wait_recv()
    down.wait()
    for k in range(len(counts)):
        part = own(0).at[pl.ds(0, u // 2)] if k in halves_sent else own(0)
        remote(part, part, send.at[k], recv.at[0, 0], me.partner).wait_send()
    for half in (0, 1):
        for slot in range(steps):
            remote(own(half), own(half), psend.at[half, slot], recv.at[0, 0], me.partner).wait_send()


FAR = (2, 1, -1, 0)
STAGES = 4


def scatter_kernel(
    n, hf, wd, wdp, y, r0, r1, r2, r3,
    wv, hv, st, acc, a0, a1, wsem, hsem, ssem, s0, s1, s2, s3, q0, q1, asem, lsem,
):
    me = Place(n)
    c = me.core
    _, _, _, _, u, units = hf.shape
    h2 = u // 2
    depth = wd.shape[1]
    wide = math.gcd(depth, 512)
    tiles = depth // wide

    greet([me.device(0, rg, rf) for rg, rf in ((0, 1), (0, -1), (1, 0), (-1, 0))])

    def weights(core, src):
        return pltpu.make_async_copy(src, wv.at[pl.ds(pl.multiple_of(core * units, 128), units)], wsem.at[core])

    weights(c, wd).start()
    weights(1 - c, wdp).start()

    places = (
        [(2, df) for df in FAR]
        + [(dg, df) for df in FAR[:3] for dg in (1, -1)]
        + [(0, df) for df in FAR]
        + [(1, 0), (-1, 0)]
    )
    count = len(places)

    def hidden(t):
        dg, df = pick(t, [p[0] for p in places]), pick(t, [p[1] for p in places])
        out = []
        for half in (0, 1):
            g, f = me.gf(half, dg, df)
            for core in (0, 1):
                out.append(
                    pltpu.make_async_copy(
                        hf.at[core, half, g, f],
                        hv.at[lax.rem(t, 2), pl.ds(half * u, u), pl.ds(core * units, units)],
                        hsem.at[lax.rem(t, 2), half, core],
                    )
                )
        return out

    for copy in hidden(jnp.int32(0)):
        copy.start()
    weights(c, wd).wait()
    weights(1 - c, wdp).wait()

    def begin(t):
        for copy in hidden(t):
            copy.wait()

        @pl.when(t + 1 < count)
        def _():
            for copy in hidden(t + 1):
                copy.start()

    def columns(i):
        return pl.ds(pl.multiple_of(i * wide, wide), wide)

    def product(t, i):
        return jnp.dot(hv[lax.rem(t, 2)], wv[:, columns(i)], preferred_element_type=F32)

    def far_send(stage, half, side, fi):
        part = st.at[stage, pl.ds(half * u + side * h2, h2)]
        return remote(
            part, r0.at[half, side, fi], ssem.at[stage, half, side], q0.at[half, side, fi],
            me.device(half, 1 - 2 * side, 0),
        )

    def near_send(stage, half, side, fi):
        part = st.at[stage, pl.ds(half * u, u)]
        return remote(
            part, r1.at[half, side, fi], ssem.at[stage, half, 0], q1.at[half, side, fi],
            me.device(half, 1 - 2 * side, 0),
        )

    def level0(i, carry):
        begin(i)

        def tile(k, carry):
            st[i, :, columns(k)] = product(i, k).astype(BF16)
            return carry

        lax.fori_loop(0, tiles, tile, 0)
        for half in (0, 1):
            for side in (0, 1):
                far_send(i, half, side, i).start()
        return carry

    lax.fori_loop(0, 4, level0, 0)

    def fetch0(half, side, fi):
        return pltpu.make_async_copy(r0.at[half, side, fi], a0.at[side, half], asem.at[side, half])

    def level1(t, fi, stage0, previous):
        for side in (0, 1):
            stage = stage0 + side
            begin(t + side)
            for half in (0, 1):
                far_send(0, half, side, fi).wait_recv()
                fetch0(half, side, fi).start()
            previous(stage, side)
            for half in (0, 1):
                fetch0(half, side, fi).wait()

            def tile(k, carry):
                total = product(t + side, k)
                parts = []
                for half in (0, 1):
                    for piece in (0, 1):
                        lo = half * u + piece * h2
                        rows = total[lo : lo + h2]
                        if piece == side:
                            rows = rows + a0[side, half, :, columns(k)].astype(F32)
                        parts.append(rows.astype(BF16))
                st[stage, :, columns(k)] = jnp.concatenate(parts, axis=0)
                return carry

            lax.fori_loop(0, tiles, tile, 0)
            for half in (0, 1):
                near_send(stage, half, side, fi).start()

    def far_sent(stage, side):
        for half in (0, 1):
            for s in (0, 1):
                far_send(stage, half, s, 0).wait_send()

    def near_sent(stage, side):
        for half in (0, 1):
            near_send(stage, half, side, 0).wait_send()

    def level1_first(i, carry):
        level1(4 + 2 * i, i, 2 * i, far_sent)
        return carry

    lax.fori_loop(0, 2, level1_first, 0)
    level1(8, 2, 0, near_sent)

    def keep(i, carry):
        t = 10 + i
        begin(t)

        def tile(k, carry):
            acc[i, :, columns(k)] = product(t, k)
            return carry

        lax.fori_loop(0, tiles, tile, 0)
        return carry

    lax.fori_loop(0, 4, keep, 0)

    def add(which, sources):
        for i, (wait, landing, lo, size) in enumerate(sources):
            wait()
            pltpu.make_async_copy(landing, a1.at[i, pl.ds(0, size)], lsem.at[i]).start()
        for i, (wait, landing, lo, size) in enumerate(sources):
            pltpu.make_async_copy(landing, a1.at[i, pl.ds(0, size)], lsem.at[i]).wait()

            def some(k, carry, i=i, lo=lo):
                rows = pl.ds(pl.multiple_of(lo + k * 16, 16), 16)
                acc[which, rows] += a1[i, pl.ds(pl.multiple_of(k * 16, 16), 16)].astype(F32)
                return carry

            lax.fori_loop(0, size // 16, some, 0)

    def rounded(which, stage):
        def some(k, carry):
            rows = pl.ds(pl.multiple_of(k * 16, 16), 16)
            st[stage, rows] = acc[which, rows].astype(BF16)
            return carry

        lax.fori_loop(0, 2 * u // 16, some, 0)

    def from_near(fi):
        return [
            (near_send(0, half, side, fi).wait_recv, r1.at[half, side, fi], half * u, u)
            for half in (0, 1)
            for side in (0, 1)
        ]

    def turn_send(half, side):
        part = st.at[2, pl.ds(half * u + side * h2, h2)]
        return remote(part, r2.at[half, side], s2.at[half, side], s0.at[half, side], me.device(half, 0, 1 - 2 * side))

    def last_send(half, side):
        part = st.at[2 + side, pl.ds(half * u, u)]
        return remote(part, r3.at[half, side], s3.at[half, side], s1.at[half, side], me.device(half, 0, 1 - 2 * side))

    add(0, from_near(0))
    near_sent(2, 0)
    rounded(0, 2)
    for half in (0, 1):
        for side in (0, 1):
            turn_send(half, side).start()

    level1(14, 3, 0, near_sent)

    near_sent(3, 1)
    for side in (0, 1):
        add(1 + side, from_near(1 + side))
    for half in (0, 1):
        for side in (0, 1):
            turn_send(half, side).wait_send()
    for side in (0, 1):
        add(
            1 + side,
            [(turn_send(half, side).wait_recv, r2.at[half, side], half * u + side * h2, h2) for half in (0, 1)],
        )
        rounded(1 + side, 2 + side)
        for half in (0, 1):
            last_send(half, side).start()

    add(3, from_near(3))
    add(
        3,
        [
            (last_send(half, side).wait_recv, r3.at[half, side], half * u, u)
            for half in (0, 1)
            for side in (0, 1)
        ],
    )
    near_sent(0, 0)
    rounded(3, 0)
    out = pltpu.make_async_copy(st.at[0], y, lsem.at[0])
    out.start()
    near_sent(1, 1)
    for half in (0, 1):
        for side in (0, 1):
            last_send(half, side).wait_send()
    out.wait()


def solution(mesh):
    n = math.isqrt(mesh.shape["tp"] // 2)
    assert n == 4 and 2 * n * n == mesh.shape["tp"]

    def step(x, w_gate, w_up, w_down):
        rows, depth = x.shape
        units = w_gate.shape[1]
        u = rows // 2
        dma = pltpu.SemaphoreType.DMA
        like = jax.ShapeDtypeStruct
        _, hidden, other_down = pl.pallas_call(
            functools.partial(gather_kernel, n),
            out_shape=(
                like((2, 2, n, n, u, depth), BF16),
                like((2, 2, n, n, u, units), BF16),
                like(w_down.shape, BF16),
            ),
            in_specs=[ANY] * 4,
            out_specs=(ANY,) * 3,
            scratch_shapes=[
                pltpu.VMEM((units // 128, depth, 256), BF16),
                pltpu.VMEM((2, 4 * u, depth), BF16),
                pltpu.VMEM((2, 4 * u, units), BF16),
                dma((32,)),
                dma((2, 17)),
                dma((2, 16)),
                dma((2, 16)),
                dma((units // 128, 2)),
                dma((2, 2, 2)),
                dma((2, 2)),
                dma((2, 2)),
                dma((1,)),
                dma((2,)),
            ],
            compiler_params=pltpu.CompilerParams(
                collective_id=0, has_side_effects=True, vmem_limit_bytes=LIMIT
            ),
            name="gather",
        )(x, w_gate, w_up, w_down)
        y, *_ = pl.pallas_call(
            functools.partial(scatter_kernel, n),
            out_shape=(
                like((rows, depth), BF16),
                like((2, 2, 4, u // 2, depth), BF16),
                like((2, 2, 4, u, depth), BF16),
                like((2, 2, u // 2, depth), BF16),
                like((2, 2, u, depth), BF16),
            ),
            in_specs=[ANY] * 3,
            out_specs=(ANY,) * 5,
            scratch_shapes=[
                pltpu.VMEM((2 * units, depth), BF16),
                pltpu.VMEM((2, 2 * u, 2 * units), BF16),
                pltpu.VMEM((STAGES, 2 * u, depth), BF16),
                pltpu.VMEM((4, 2 * u, depth), F32),
                pltpu.VMEM((2, 2, u // 2, depth), BF16),
                pltpu.VMEM((4, u, depth), BF16),
                dma((2,)),
                dma((2, 2, 2)),
                dma((STAGES, 2, 2)),
                dma((2, 2)),
                dma((2, 2)),
                dma((2, 2)),
                dma((2, 2)),
                dma((2, 2, 4)),
                dma((2, 2, 4)),
                dma((2, 2)),
                dma((4,)),
            ],
            compiler_params=pltpu.CompilerParams(
                collective_id=1, has_side_effects=True, vmem_limit_bytes=LIMIT
            ),
            name="scatter",
        )(hidden, w_down, other_down)
        return y

    return jax.shard_map(
        step,
        mesh=mesh,
        in_specs=(P(("dp", "tp"), None), P(None, "tp"), P(None, "tp"), P("tp", None)),
        out_specs=P(("dp", "tp"), None),
        check_vma=False,
    )
```

time: 875 us -> 497 us (0.57)
  waiting for transfers between devices: 535 us -> 0 us
  Pallas kernels: 0 us -> 494 us
  matrix products: 326 us -> 0 us
  between operations: 13.4 us -> 0.02 us
    pallas_call x0 -> x2, Pallas kernels: none -> 494 us  [the longest x1 280 us: step(): pl.pallas_call(functools.partial(gather_kernel, n), out_shape=(like((2, 2...]
    dot_general x3 -> x0, matrix products: 326 us -> none  [the longest x1 112 us: step(): up = jnp.dot(rows, w_up, preferred_element_type=jnp.float32)]
    unnamed x3 -> x0, waiting for transfers between devices: 311 us -> none
    all_gather x1 -> x0, waiting for transfers between devices: 224 us -> none  [step(): rows = lax.all_gather(x, 'tp', axis=0, tiled=True)]
  transfers between devices with their start and end apart: 2 -> 0, of which waited for: 2 -> 0; matrix products, arithmetic and copies ran while one was open for 0% -> 0% of each run, Pallas kernels for 0% -> 0%
where the time goes in v1:
time: 497 us
  Pallas kernels  494 us (99%)
    pallas_call x1, Pallas kernels, step(): pl.pallas_call(functools.partial(gather_kernel, n), out_shape=(like((2, 2...  280 us
    pallas_call x1, Pallas kernels, step(): pl.pallas_call(functools.partial(scatter_kernel, n), out_shape=(like((row...  214 us

profile of v1, /device:TPU:97, one launch (start us, length us, event | category | flops | bytes accessed | tf_op | source)
XLA Modules:
  0.0 496.9 jit_solution(14402414325570020537)
XLA Ops:
  0.0 279.7 %gather.1 = (bf16[2,2,4,4,128,4608]{5,4,3,2,1,0:T(8,128)(2,1)}, bf16[2,2,4,4,128,1152]{5,4,3,2,1,0:T(8,128)(2,1)}, bf16[1152,4608]{1,0:T(8,128)(2,1)}) custom-call(bf16[256,4608]{1,0:T(8,128)(2,1)} %x.1, bf16[4608,1152]{1,0:T(8,128)(2,1)} %wg.1, bf16[4608,1152]{1,0:T(8,128)(2,1)} %wu.1, bf16[1152,4608]{1,0:T(8,128)(2,1)} %wd.3), custom_call_target="tpu_custom_call" | custom-call | tf_op jit(solution)/shard_map/gather/pallas_call | solution.py:500
  279.7 214.0 %scatter.1 = (bf16[256,4608]{1,0:T(8,128)(2,1)}, bf16[2,2,4,64,4608]{4,3,2,1,0:T(8,128)(2,1)}, bf16[2,2,4,128,4608]{4,3,2,1,0:T(8,128)(2,1)}, bf16[2,2,64,4608]{3,2,1,0:T(8,128)(2,1)}, bf16[2,2,128,4608]{3,2,1,0:T(8,128)(2,1)}) custom-call(bf16[2,2,4,4,128,1152]{5,4,3,2,1,0:T(8,128)(2,1)} %get-tuple-element.8.hf, bf16[1152,4608]{1,0:T(8,128)(2,1)} %wd.3, ...), custom_call_target="tpu_custom_call" | custom-call | tf_op jit(solution)/shard_map/scatter/pallas_call | solution.py:529
  493.7 3.2 copy.6

commit v2 on v0

v2 whole, which is shorter than its diff:
```python
import functools
import math

import jax
import jax.numpy as jnp
from jax import lax
from jax.experimental import pallas as pl
from jax.experimental.pallas import tpu as pltpu
from jax.sharding import PartitionSpec as P

MESH = pl.DeviceIdType.MESH
BF16, F32 = jnp.bfloat16, jnp.float32
ANY = pl.BlockSpec(memory_space=pl.ANY)
LIMIT = 67043328

ORDER = (
    (0, 0), (0, -1), (0, 1), (-1, 0), (1, 0), (0, 2), (-1, -1), (1, -1),
    (-1, 1), (1, 1), (-1, 2), (1, 2), (2, 0), (2, 1), (2, -1), (2, 2),
)
SLOT = {place: i for i, place in enumerate(ORDER)}
SECOND_HALF = len(ORDER)


def pick(index, values):
    out = jnp.int32(values[0])
    for i, v in enumerate(values[1:], 1):
        out = jnp.where(index == i, jnp.int32(v), out)
    return out


class Place:
    def __init__(self, n):
        t = lax.axis_index("tp")
        self.n = n
        self.core = lax.rem(t, 2)
        self.partner = t + 1 - 2 * self.core
        self.y = lax.rem(lax.div(t, 2), n)
        self.x = lax.div(t, 2 * n)

    def gf(self, half, rg=0, rf=0):
        g, f = (self.x, self.y) if half == 0 else (self.y, self.x)
        return lax.rem(g + rg + self.n, self.n), lax.rem(f + rf + self.n, self.n)

    def device(self, half, rg, rf):
        g, f = self.gf(half, rg, rf)
        x, y = (g, f) if half == 0 else (f, g)
        return (x * self.n + y) * 2 + self.core


def remote(src, dst, send, recv, device):
    return pltpu.make_async_remote_copy(
        src_ref=src, dst_ref=dst, send_sem=send, recv_sem=recv, device_id={"tp": device}, device_id_type=MESH
    )


def greet(devices):
    barrier = pltpu.get_barrier_semaphore()
    for d in devices:
        pl.semaphore_signal(barrier, inc=1, device_id={"tp": d}, device_id_type=MESH)
    pl.semaphore_wait(barrier, len(devices))


EARLY = (0, 1)


def kernel(
    n, x, wg, wu, wd, y, xg, hf, r0, r1, r2, r3,
    wdv, hv, st, send, recv, psend, precv, wsem, xsem, hsend, hlocal, hrecv, dsem,
    hsem, ssem, q0, q1, q2, q3, lsem,
):
    me = Place(n)
    c = me.core
    rows, depth = x.shape
    u = rows // 2
    units = wg.shape[1]
    h2 = u // 2
    wide = math.gcd(depth, 512)

    def block(owner_core, half, rg, rf):
        g, f = me.gf(half, rg, rf)
        return xg.at[owner_core, half, g, f]

    counts = []

    def push(src, dst, half, device, slot):
        k = len(counts)
        counts.append(src)
        remote(src, dst, send.at[k], recv.at[half, slot], device).start()

    halves_sent = []

    def own(half):
        return x.at[pl.ds(half * u, u)]

    def forward(half, place):
        rg, rf = place
        mine = block(c, half, rg, rf)
        if place == (0, 0):
            src = own(half)
            push(src, mine, half, me.device(half, 0, 1), SLOT[(0, -1)])
            push(src, mine, half, me.device(half, 0, -1), SLOT[(0, 1)])
            push(src, mine, half, me.device(half, 1, 0), SLOT[(-1, 0)])
            push(src, mine, half, me.device(half, -1, 0), SLOT[(1, 0)])
        else:
            src = mine
        if place == (0, -1):
            part = mine.at[pl.ds(0, u // 2)]
            halves_sent.append(len(counts))
            push(part, part, half, me.device(half, 0, 1), SLOT[(0, 2)])
        if place == (0, 1):
            part = mine.at[pl.ds(u // 2, u // 2)]
            halves_sent.append(len(counts))
            push(part, part, half, me.device(half, 0, -1), SECOND_HALF)
        if rg == 0 and rf != 0:
            push(mine, mine, half, me.device(half, 1, 0), SLOT[(-1, rf)])
            push(mine, mine, half, me.device(half, -1, 0), SLOT[(1, rf)])
        if rg == -1 and rf in (0, -1):
            push(mine, mine, half, me.device(half, 1, 0), SLOT[(2, rf)])
        if rg == 1 and rf in (1, 2):
            push(mine, mine, half, me.device(half, -1, 0), SLOT[(2, rf)])
        remote(src, mine, psend.at[half, SLOT[place]], precv.at[half, SLOT[place]], me.partner).start()

    def arrived(half, place):
        mine = block(c, half, *place)
        if place == (0, 2):
            for slot, lo in ((SLOT[place], 0), (SECOND_HALF, u // 2)):
                part = mine.at[pl.ds(lo, u // 2)]
                remote(part, part, send.at[0], recv.at[half, slot], me.partner).wait_recv()
        else:
            remote(mine, mine, send.at[0], recv.at[half, SLOT[place]], me.partner).wait_recv()

    def handed_over(half, slot, rg, rf):
        theirs = block(1 - c, half, rg, rf)
        remote(theirs, theirs, send.at[0], precv.at[half, slot], me.partner).wait_recv()

    greet(
        [me.partner]
        + [me.device(0, rg, rf) for rg, rf in ((0, 1), (0, -1), (1, 0), (-1, 0))]
    )
    for half in (0, 1):
        forward(half, (0, 0))
    my_units = wdv.at[pl.ds(pl.multiple_of(c * units, 128), units)]
    down = remote(wd, my_units, dsem.at[0], dsem.at[1], me.partner)
    down_here = pltpu.make_async_copy(wd, my_units, dsem.at[2])

    def hidden(t, place):
        out = []
        for half in (0, 1):
            g, f = me.gf(half, *place)
            for core in (0, 1):
                out.append(
                    pltpu.make_async_copy(
                        hf.at[core, half, g, f],
                        hv.at[lax.rem(t, 2), pl.ds(half * u, u), pl.ds(core * units, units)],
                        hsem.at[lax.rem(t, 2), half, core],
                    )
                )
        return out

    def columns(i):
        return pl.ds(pl.multiple_of(i * wide, wide), wide)

    def product(t, i):
        return jnp.dot(hv[lax.rem(t, 2)], wdv[:, columns(i)], preferred_element_type=F32)

    def hidden_came(slot, rg, rf):
        for half in (0, 1):
            g, f = me.gf(half, rg, rf)
            landed = hf.at[1 - c, half, g, f]
            remote(landed, landed, send.at[0], hrecv.at[half, slot], me.partner).wait_recv()

    def over(body):
        def tile(k, carry):
            body(k)
            return carry

        lax.fori_loop(0, depth // wide, tile, 0)

    def to(half, dg, df):
        return me.device(half, df, dg)

    def far_send(ref, stage, half, side, fi):
        part = ref.at[pl.ds(half * u + side * h2, h2)]
        return remote(
            part, r0.at[half, side, fi], ssem.at[stage, half, side], q0.at[half, side, fi], to(half, 1 - 2 * side, 0)
        )

    def level0(ref, stage, t, fi):
        def body(k):
            ref[:, columns(k)] = product(t, k).astype(BF16)

        over(body)
        for half in (0, 1):
            for side in (0, 1):
                far_send(ref, stage, half, side, fi).start()

    def early_place(i):
        return pick(i, EARLY), 2

    def gather(wv, xb, hb):
        tiles = units // 128

        def tile_rows(core, half):
            return pl.ds(pl.multiple_of((core * 2 + half) * u, u), u)

        def tile_copy(slot, core, half, rg, rf):
            return pltpu.make_async_copy(
                block(core, half, rg, rf), xb.at[slot, tile_rows(core, half)], xsem.at[slot, core, half]
            )

        for half in (0, 1):
            pltpu.make_async_copy(own(half), xb.at[0, tile_rows(c, half)], xsem.at[0, c, half]).start()

        def weights(j, part):
            w = (wg, wu)[part]
            return pltpu.make_async_copy(
                w.at[:, pl.ds(pl.multiple_of(j * 128, 128), 128)],
                wv.at[j, :, pl.ds(part * 128, 128)],
                wsem.at[j, part],
            )

        def start_weights(j, carry):
            weights(j, 0).start()
            weights(j, 1).start()
            return carry

        lax.fori_loop(0, tiles, start_weights, 0)
        for half in (0, 1):
            handed_over(half, 0, 0, 0)
            tile_copy(0, 1 - c, half, 0, 0).start()
        down.start()
        down_here.start()

        group = math.gcd(tiles, 3)
        look, fetch = tiles // group // 3, 2 * (tiles // group) // 3
        steps = len(ORDER)

        def offsets(s):
            return pick(s, [p[0] for p in ORDER]), pick(s, [p[1] for p in ORDER])

        def hidden_copies(slot, half, rg, rf, s):
            g, f = me.gf(half, rg, rf)
            mine = pltpu.make_async_copy(
                hb.at[slot, tile_rows(c, half)], hf.at[c, half, g, f], hlocal.at[slot, half]
            )
            theirs = remote(
                hb.at[slot, tile_rows(1 - c, half)], hf.at[c, half, g, f],
                hsend.at[slot, half], hrecv.at[half, s], me.partner,
            )
            return mine, theirs

        def early_fetch(i):
            rg, rf = early_place(i)
            hidden_came(pick(i, [SLOT[(df, 2)] for df in EARLY]), rg, rf)
            for copy in hidden(i, (rg, rf)):
                copy.start()

        def step(s, carry):
            slot = lax.rem(s, 2)
            rg, rf = offsets(s)
            ng, nf = offsets(s + 1)
            for core in (0, 1):
                for half in (0, 1):
                    tile_copy(slot, core, half, rg, rf).wait()

            @pl.when(s >= 2)
            def _():
                for half in (0, 1):
                    mine, theirs = hidden_copies(slot, half, rg, rf, s)
                    mine.wait()
                    theirs.wait_send()

            def some_tiles(i, carry):
                @pl.when(s == 0)
                def _():
                    for q in range(group):
                        weights(i * group + q, 0).wait()
                        weights(i * group + q, 1).wait()

                @pl.when(i == look)
                def _():
                    for k in range(1, steps):

                        @pl.when(s == k - 1)
                        def _():
                            for half in (0, 1):
                                arrived(half, ORDER[k])
                                forward(half, ORDER[k])

                @pl.when(i == fetch)
                def _():
                    @pl.when(s < steps - 1)
                    def _():
                        for half in (0, 1):
                            tile_copy(1 - slot, c, half, ng, nf).start()
                        for half in (0, 1):
                            handed_over(half, s + 1, ng, nf)
                            tile_copy(1 - slot, 1 - c, half, ng, nf).start()

                    @pl.when(s == 11)
                    def _():
                        down.wait_recv()
                        down_here.wait()
                        early_fetch(jnp.int32(0))

                    @pl.when(s == 13)
                    def _():
                        early_fetch(jnp.int32(1))

                both = jnp.dot(xb[slot], wv[i * group], preferred_element_type=F32)
                for q in range(group):
                    gate, up = both[:, :128], both[:, 128:]
                    if q + 1 < group:
                        both = jnp.dot(xb[slot], wv[i * group + q + 1], preferred_element_type=F32)
                    j = i * group + q
                    hb[slot, :, pl.ds(pl.multiple_of(j * 128, 128), 128)] = (jax.nn.gelu(gate) * up).astype(BF16)
                return carry

            lax.fori_loop(0, tiles // group, some_tiles, 0)
            for half in (0, 1):
                mine, theirs = hidden_copies(slot, half, rg, rf, s)
                mine.start()
                theirs.start()

            def early(i, carry):
                for copy in hidden(i, early_place(i)):
                    copy.wait()

                level0(st.at[i], i, i, lax.rem(pick(i, EARLY) + n, n))
                return carry

            first = jnp.where(s == 13, 1, 0)
            lax.fori_loop(first, jnp.where(s == 13, 2, jnp.where(s == 11, 1, 0)), early, 0)
            return carry

        lax.fori_loop(0, steps, step, 0)
        for slot in (0, 1):
            for half in (0, 1):
                mine, theirs = hidden_copies(slot, half, 0, 0, 0)
                mine.wait()
                theirs.wait_send()

    pl.run_scoped(
        gather,
        pltpu.VMEM((units // 128, depth, 256), BF16),
        pltpu.VMEM((2, 4 * u, depth), BF16),
        pltpu.VMEM((2, 4 * u, units), BF16),
    )

    def scatter(acc, a0, a1, more):
        stages = [st.at[0], st.at[1], more.at[0], more.at[1], more.at[2]]
        near = (1, 2, -1, 0)
        places = (
            [(2, -1), (2, 2)]
            + [(dg, df) for df in near[:3] for dg in (1, -1)]
            + [(0, df) for df in (2, 1, -1, 0)]
            + [(1, 0), (-1, 0)]
        )
        done = {"t": 0}

        def fetch(i):
            dg, df = places[i]
            hidden_came(SLOT[(df, dg)], df, dg)
            for copy in hidden(jnp.int32(i + 1), (df, dg)):
                copy.start()

        fetch(0)

        def begin(place):
            i = done["t"]
            assert places[i] == place
            done["t"] = i + 1
            for copy in hidden(jnp.int32(i + 1), (place[1], place[0])):
                copy.wait()
            if i + 1 < len(places):
                fetch(i + 1)
            return jnp.int32(i + 1)

        pending = {
            i: [(lambda i=i, half=half, side=side: far_send(stages[i], i, half, side, 0)) for half in (0, 1) for side in (0, 1)]
            for i in range(4)
        }

        def free(stage):
            for copy in pending.pop(stage, []):
                copy().wait_send()

        for stage, df in ((2, -1), (3, 2)):
            t = begin((2, df))
            level0(stages[stage], stage, t, df % n)

        def near_send(stage, half, side, fi):
            part = stages[stage].at[pl.ds(half * u, u)]
            return remote(
                part, r1.at[half, side, fi], ssem.at[stage, half, 0], q1.at[half, side, fi], to(half, 1 - 2 * side, 0)
            )

        def level1(df, used):
            fi = df % n
            for side, stage in enumerate(used):
                t = begin((1 - 2 * side, df))
                fetches = []
                for half in (0, 1):
                    far_send(st.at[0], 0, half, side, fi).wait_recv()
                    copy = pltpu.make_async_copy(r0.at[half, side, fi], a0.at[half], lsem.at[half])
                    copy.start()
                    fetches.append(copy)
                free(stage)
                for copy in fetches:
                    copy.wait()

                def body(k, t=t, side=side, stage=stage):
                    total = product(t, k)
                    parts = []
                    for half in (0, 1):
                        for piece in (0, 1):
                            lo = half * u + piece * h2
                            rows = total[lo : lo + h2]
                            if piece == side:
                                rows = rows + a0[half, :, columns(k)].astype(F32)
                            parts.append(rows.astype(BF16))
                    stages[stage][:, columns(k)] = jnp.concatenate(parts, axis=0)

                over(body)
                for half in (0, 1):
                    near_send(stage, half, side, fi).start()
                pending[stage] = [
                    (lambda stage=stage, side=side, half=half: near_send(stage, half, side, 0)) for half in (0, 1)
                ]

        level1(1, (4, 0))
        level1(2, (1, 2))
        level1(-1, (3, 4))

        for i, df in enumerate((2, 1, -1, 0)):
            t = begin((0, df))

            def body(k, t=t, i=i):
                acc[i, :, columns(k)] = product(t, k)

            over(body)

        def add(which, sources):
            copies = []
            for i, (wait, landing, lo, size) in enumerate(sources):
                wait()
                copy = pltpu.make_async_copy(landing, a1.at[i, pl.ds(0, size)], lsem.at[i])
                copy.start()
                copies.append(copy)
            for i, (wait, landing, lo, size) in enumerate(sources):
                copies[i].wait()

                def some(k, carry, i=i, lo=lo):
                    rows = pl.ds(pl.multiple_of(lo + k * 16, 16), 16)
                    acc[which, rows] += a1[i, pl.ds(pl.multiple_of(k * 16, 16), 16)].astype(F32)
                    return carry

                lax.fori_loop(0, size // 16, some, 0)

        def rounded(which, stage):
            free(stage)

            def some(k, carry):
                rows = pl.ds(pl.multiple_of(k * 16, 16), 16)
                stages[stage][rows] = acc[which, rows].astype(BF16)
                return carry

            lax.fori_loop(0, 2 * u // 16, some, 0)

        def from_near(df):
            fi = df % n
            return [
                (near_send(0, half, side, fi).wait_recv, r1.at[half, side, fi], half * u, u)
                for half in (0, 1)
                for side in (0, 1)
            ]

        def turn_send(half, side):
            part = stages[0].at[pl.ds(half * u + side * h2, h2)]
            return remote(part, r2.at[half, side], ssem.at[0, half, side], q2.at[half, side], to(half, 0, 1 - 2 * side))

        def last_send(half, side):
            part = stages[3 + side].at[pl.ds(half * u, u)]
            return remote(part, r3.at[half, side], ssem.at[3 + side, half, 0], q3.at[half, side], to(half, 0, 1 - 2 * side))

        add(0, from_near(2))
        rounded(0, 0)
        for half in (0, 1):
            for side in (0, 1):
                turn_send(half, side).start()
        pending[0] = [(lambda half=half, side=side: turn_send(half, side)) for half in (0, 1) for side in (0, 1)]

        level1(0, (1, 2))

        for side in (0, 1):
            add(1 + side, from_near(1 - 2 * side))
        for side in (0, 1):
            add(
                1 + side,
                [(turn_send(half, side).wait_recv, r2.at[half, side], half * u + side * h2, h2) for half in (0, 1)],
            )
            rounded(1 + side, 3 + side)
            for half in (0, 1):
                last_send(half, side).start()
            pending[3 + side] = [(lambda half=half, side=side: last_send(half, side)) for half in (0, 1)]

        add(3, from_near(0))
        add(
            3,
            [
                (last_send(half, side).wait_recv, r3.at[half, side], half * u, u)
                for half in (0, 1)
                for side in (0, 1)
            ],
        )
        rounded(3, 0)
        out = pltpu.make_async_copy(stages[0], y, lsem.at[0])
        out.start()
        for stage in (1, 2, 3, 4):
            free(stage)
        out.wait()

    pl.run_scoped(
        scatter,
        pltpu.VMEM((4, 2 * u, depth), F32),
        pltpu.VMEM((2, h2, depth), BF16),
        pltpu.VMEM((4, u, depth), BF16),
        pltpu.VMEM((3, 2 * u, depth), BF16),
    )

    down.wait_send()
    for k in range(len(counts)):
        part = own(0).at[pl.ds(0, h2)] if k in halves_sent else own(0)
        remote(part, part, send.at[k], recv.at[0, 0], me.partner).wait_send()
    for half in (0, 1):
        for slot in range(len(ORDER)):
            remote(own(half), own(half), psend.at[half, slot], recv.at[0, 0], me.partner).wait_send()


def solution(mesh):
    n = math.isqrt(mesh.shape["tp"] // 2)
    assert n == 4 and 2 * n * n == mesh.shape["tp"]

    def step(x, w_gate, w_up, w_down):
        rows, depth = x.shape
        units = w_gate.shape[1]
        u = rows // 2
        dma = pltpu.SemaphoreType.DMA
        like = jax.ShapeDtypeStruct
        y, *_ = pl.pallas_call(
            functools.partial(kernel, n),
            out_shape=(
                like((rows, depth), BF16),
                like((2, 2, n, n, u, depth), BF16),
                like((2, 2, n, n, u, units), BF16),
                like((2, 2, n, u // 2, depth), BF16),
                like((2, 2, n, u, depth), BF16),
                like((2, 2, u // 2, depth), BF16),
                like((2, 2, u, depth), BF16),
            ),
            in_specs=[ANY] * 4,
            out_specs=(ANY,) * 7,
            scratch_shapes=[
                pltpu.VMEM((2 * units, depth), BF16),
                pltpu.VMEM((2, 2 * u, 2 * units), BF16),
                pltpu.VMEM((2, 2 * u, depth), BF16),
                dma((32,)),
                dma((2, 17)),
                dma((2, 16)),
                dma((2, 16)),
                dma((units // 128, 2)),
                dma((2, 2, 2)),
                dma((2, 2)),
                dma((2, 2)),
                dma((2, 16)),
                dma((3,)),
                dma((2, 2, 2)),
                dma((5, 2, 2)),
                dma((2, 2, n)),
                dma((2, 2, n)),
                dma((2, 2)),
                dma((2, 2)),
                dma((4,)),
            ],
            compiler_params=pltpu.CompilerParams(
                collective_id=0, has_side_effects=True, vmem_limit_bytes=LIMIT
            ),
            name="block",
        )(x, w_gate, w_up, w_down)
        return y

    return jax.shard_map(
        step,
        mesh=mesh,
        in_specs=(P(("dp", "tp"), None), P(None, "tp"), P(None, "tp"), P("tp", None)),
        out_specs=P(("dp", "tp"), None),
        check_vma=False,
    )
```

time: 875 us -> 466 us (0.53)
  waiting for transfers between devices: 535 us -> 0 us
  Pallas kernels: 0 us -> 462 us
  matrix products: 326 us -> 0 us
  between operations: 13.4 us -> 0.01 us
    pallas_call x0 -> x1, Pallas kernels: none -> 462 us  [step(): pl.pallas_call(functools.partial(kernel, n), out_shape=(like((rows, depth...]
    dot_general x3 -> x0, matrix products: 326 us -> none  [the longest x1 112 us: step(): up = jnp.dot(rows, w_up, preferred_element_type=jnp.float32)]
    unnamed x3 -> x0, waiting for transfers between devices: 311 us -> none
    all_gather x1 -> x0, waiting for transfers between devices: 224 us -> none  [step(): rows = lax.all_gather(x, 'tp', axis=0, tiled=True)]
  transfers between devices with their start and end apart: 2 -> 0, of which waited for: 2 -> 0; matrix products, arithmetic and copies ran while one was open for 0% -> 0% of each run, Pallas kernels for 0% -> 0%
where the time goes in v2:
time: 466 us
  Pallas kernels  462 us (99%)
    pallas_call x1, Pallas kernels, step(): pl.pallas_call(functools.partial(kernel, n), out_shape=(like((rows, depth...  462 us

profile of v2, /device:TPU:97, one launch (start us, length us, event | category | flops | bytes accessed | tf_op | source)
XLA Modules:
  0.0 465.5 jit_solution(15101139553369916588)
XLA Ops:
  0.0 462.3 %block.1 = (bf16[256,4608]{1,0:T(8,128)(2,1)}, bf16[2,2,4,4,128,4608]{5,4,3,2,1,0:T(8,128)(2,1)}, bf16[2,2,4,4,128,1152]{5,4,3,2,1,0:T(8,128)(2,1)}, bf16[2,2,4,...) custom-call(bf16[256,4608]{1,0:T(8,128)(2,1)} %x.1, ...), custom_call_target="tpu_custom_call" | custom-call | tf_op jit(solution)/shard_map/block/pallas_call | solution.py:550
  462.3 3.2 copy.6
